TPU v7x, 16 devices: a 4x2x1 block of a 4x4x8 slice. The times are simulated.
16 devices in a mesh: dp: 2 (over y, z), stage: 8 (over x, core).
Axes of the slice: x: 4, y: 2, z: 1, core: 2. Of those that a mesh axis runs over, the one named last changes fastest.
The devices are a block of a 4x4x8 slice.
Arguments:
- tokens_in: bfloat16 [16, 512, 1024], P('dp'), parts along dimension 0
- targets: bfloat16 [16, 512, 1024], P('dp'), parts along dimension 0
- w_in: bfloat16 [16, 1024, 4096], P('stage')
- w_out: bfloat16 [16, 4096, 1024], P('stage')
- norm_gains: float32 [16, 1024], P('stage')
Outputs:
- output 1: float32 [32, 1024, 4096], P(('dp', 'stage')), parts along dimension 0
- output 2: float32 [32, 4096, 1024], P(('dp', 'stage')), parts along dimension 0
- output 3: float32 [32, 1024], P(('dp', 'stage')), parts along dimension 0
- output 4: float32 [2], P('dp'), parts along dimension 0
There are 2 independent parts. A program takes and returns all parts, laid end to end along the dimension named above; an argument that names none is the same for every part.
All inputs are finite; a program needn't handle non-finite values.
Results may differ from a plain program's by a relative error of at most 0.00514443.
Values are sent between devices in bfloat16 or wider.
A program may use at most 768 MiB of HBM per device.

v0:
```python
import jax
import jax.numpy as jnp
from jax import lax
from jax.sharding import PartitionSpec as P

EPSILON = 1e-6


def norm_scale(x_f32, gain_vec):
    inv_rms = lax.rsqrt(jnp.mean(x_f32 * x_f32, axis=-1, keepdims=True) + EPSILON)
    return x_f32 * inv_rms * gain_vec


def layer_forward(x_act, first_w, second_w, gain_vec):
    x_f32 = x_act.astype(jnp.float32)
    normed = norm_scale(x_f32, gain_vec).astype(jnp.bfloat16)
    pre_act = jnp.dot(normed, first_w, preferred_element_type=jnp.float32)
    hidden = jax.nn.gelu(pre_act).astype(jnp.bfloat16)
    out_f32 = jnp.dot(hidden, second_w, preferred_element_type=jnp.float32)
    return (x_f32 + out_f32).astype(jnp.bfloat16)


def layer_backward(x_act, grad_h, first_w, second_w, gain_vec):
    x_f32 = x_act.astype(jnp.float32)
    normed_f32, norm_vjp = jax.vjp(norm_scale, x_f32, gain_vec)
    normed = normed_f32.astype(jnp.bfloat16)
    pre_act = jnp.dot(normed, first_w, preferred_element_type=jnp.float32)
    hidden_f32, gelu_vjp = jax.vjp(jax.nn.gelu, pre_act)
    hidden = hidden_f32.astype(jnp.bfloat16)
    grad_second = jnp.einsum('tf,td->fd', hidden, grad_h, preferred_element_type=jnp.float32)
    grad_hidden = jnp.einsum('td,fd->tf', grad_h, second_w, preferred_element_type=jnp.float32)
    grad_pre = gelu_vjp(grad_hidden)[0].astype(jnp.bfloat16)
    grad_first = jnp.einsum('td,tf->df', normed, grad_pre, preferred_element_type=jnp.float32)
    grad_normed = jnp.einsum('tf,df->td', grad_pre, first_w, preferred_element_type=jnp.float32)
    grad_x_norm, grad_gain = norm_vjp(grad_normed)
    grad_x = (grad_h.astype(jnp.float32) + grad_x_norm).astype(jnp.bfloat16)
    return grad_x, grad_first, grad_second, grad_gain


def segment_forward(x_act, first_w, second_w, gain_rows):
    kept_list = []
    for layer_idx in range(first_w.shape[0]):
        kept_list.append(x_act)
        x_act = layer_forward(x_act, first_w[layer_idx], second_w[layer_idx], gain_rows[layer_idx])
    return x_act, jnp.stack(kept_list)


def segment_backward(kept_inputs, grad_h, first_w, second_w, gain_rows, grad_sums):
    layer_count = first_w.shape[0]
    first_list = [None] * layer_count
    second_list = [None] * layer_count
    gain_list = [None] * layer_count
    for layer_idx in reversed(range(layer_count)):
        grad_h, grad_first, grad_second, grad_gain = layer_backward(
            kept_inputs[layer_idx], grad_h, first_w[layer_idx], second_w[layer_idx], gain_rows[layer_idx])
        first_list[layer_idx] = grad_first
        second_list[layer_idx] = grad_second
        gain_list[layer_idx] = grad_gain
    new_sums = (grad_sums[0] + jnp.stack(first_list), grad_sums[1] + jnp.stack(second_list),
                grad_sums[2] + jnp.stack(gain_list))
    return grad_h, new_sums


def store_inputs(buffer_all, kept_inputs, mb_index, is_valid):
    old_rows = lax.dynamic_index_in_dim(buffer_all, mb_index, 1, keepdims=False)
    return lax.dynamic_update_index_in_dim(buffer_all, jnp.where(is_valid, kept_inputs, old_rows), mb_index, 1)


def solution(mesh):
    stages = mesh.shape['stage']
    down_perm = [(src_idx, src_idx + 1) for src_idx in range(stages - 1)]
    up_perm = [(src_idx + 1, src_idx) for src_idx in range(stages - 1)]

    def device_step(tokens, targets, w_in, w_out, norm_gains):
        stage_idx = lax.axis_index('stage')
        micro_count, tokens_mb, d_model = tokens.shape
        d_ff = w_in.shape[2]
        segment = w_in.shape[0] // 2
        tick_count = micro_count + 2 * stages - 1
        is_first = stage_idx == 0
        is_last = stage_idx == stages - 1
        up_offset = 2 * stages - 1 - stage_idx
        down_weights = (w_in[:segment], w_out[:segment], norm_gains[:segment])
        up_weights = (w_in[segment:], w_out[segment:], norm_gains[segment:])
        zero_act = jnp.zeros((tokens_mb, d_model), jnp.bfloat16)
        zero_saved = jnp.zeros((segment,) + tokens.shape, jnp.bfloat16)

        def run_down(x_act):
            return segment_forward(x_act, down_weights[0], down_weights[1], down_weights[2])

        def run_up(x_act):
            return segment_forward(x_act, up_weights[0], up_weights[1], up_weights[2])

        def skip_forward(x_act):
            return x_act, jnp.zeros((segment, tokens_mb, d_model), jnp.bfloat16)

        def forward_tick(loop_state, tick_idx):
            in_down, in_up, saved_down, saved_up, finals = loop_state
            mb_down = tick_idx - stage_idx
            mb_up = tick_idx - up_offset
            ok_down = (mb_down >= 0) & (mb_down < micro_count)
            ok_up = (mb_up >= 0) & (mb_up < micro_count)
            idx_down = jnp.clip(mb_down, 0, micro_count - 1)
            idx_up = jnp.clip(mb_up, 0, micro_count - 1)
            in_down = jnp.where(is_first, lax.dynamic_index_in_dim(tokens, idx_down, 0, keepdims=False), in_down)
            out_down, kept_down = lax.cond(ok_down, run_down, skip_forward, in_down)
            out_up, kept_up = lax.cond(ok_up, run_up, skip_forward, in_up)
            saved_down = store_inputs(saved_down, kept_down, idx_down, ok_down)
            saved_up = store_inputs(saved_up, kept_up, idx_up, ok_up)
            old_final = lax.dynamic_index_in_dim(finals, idx_up, 0, keepdims=False)
            finals = lax.dynamic_update_index_in_dim(
                finals, jnp.where(ok_up & is_first, out_up, old_final), idx_up, 0)
            recv_down = lax.ppermute(out_down, 'stage', down_perm)
            recv_up = lax.ppermute(out_up, 'stage', up_perm)
            next_up = jnp.where(is_last, out_down, recv_up)
            return (recv_down, next_up, saved_down, saved_up, finals), None

        fwd_init = (zero_act, zero_act, zero_saved, zero_saved, jnp.zeros(tokens.shape, jnp.bfloat16))
        fwd_state, _ = lax.scan(forward_tick, fwd_init, jnp.arange(tick_count))
        saved_down, saved_up, finals = fwd_state[2], fwd_state[3], fwd_state[4]
        error_f32 = finals.astype(jnp.float32) - targets.astype(jnp.float32)
        seed_grads = (error_f32 * (2.0 / (micro_count * tokens_mb))).astype(jnp.bfloat16)
        sse_local = jnp.where(is_first, jnp.sum(error_f32 * error_f32), 0.0)
        loss_value = lax.psum(sse_local, 'stage') / (micro_count * tokens_mb * d_model)

        def run_down_back(operand):
            return segment_backward(operand[1], operand[0], down_weights[0], down_weights[1],
                                    down_weights[2], operand[2])

        def run_up_back(operand):
            return segment_backward(operand[1], operand[0], up_weights[0], up_weights[1],
                                    up_weights[2], operand[2])

        def skip_backward(operand):
            return jnp.zeros_like(operand[0]), operand[2]

        def backward_tick(loop_state, tick_idx):
            grad_up_in, grad_down_in, sums_up, sums_down = loop_state
            mb_up = tick_idx - stage_idx
            mb_down = tick_idx - up_offset
            ok_up = (mb_up >= 0) & (mb_up < micro_count)
            ok_down = (mb_down >= 0) & (mb_down < micro_count)
            idx_up = jnp.clip(mb_up, 0, micro_count - 1)
            idx_down = jnp.clip(mb_down, 0, micro_count - 1)
            grad_up_in = jnp.where(is_first, lax.dynamic_index_in_dim(seed_grads, idx_up, 0, keepdims=False),
                                   grad_up_in)
            kept_up = lax.dynamic_index_in_dim(saved_up, idx_up, 1, keepdims=False)
            kept_down = lax.dynamic_index_in_dim(saved_down, idx_down, 1, keepdims=False)
            grad_up_out, sums_up = lax.cond(ok_up, run_up_back, skip_backward, (grad_up_in, kept_up, sums_up))
            grad_down_out, sums_down = lax.cond(ok_down, run_down_back, skip_backward,
                                                (grad_down_in, kept_down, sums_down))
            recv_up = lax.ppermute(grad_up_out, 'stage', down_perm)
            recv_down = lax.ppermute(grad_down_out, 'stage', up_perm)
            next_down = jnp.where(is_last, grad_up_out, recv_down)
            return (recv_up, next_down, sums_up, sums_down), None

        zero_sums = (jnp.zeros((segment, d_model, d_ff), jnp.float32),
                     jnp.zeros((segment, d_ff, d_model), jnp.float32),
                     jnp.zeros((segment, d_model), jnp.float32))
        back_init = (zero_act, zero_act, zero_sums, zero_sums)
        back_state, _ = lax.scan(backward_tick, back_init, jnp.arange(tick_count))
        sums_up, sums_down = back_state[2], back_state[3]
        grad_w_in = jnp.concatenate([sums_down[0], sums_up[0]], axis=0)
        grad_w_out = jnp.concatenate([sums_down[1], sums_up[1]], axis=0)
        grad_gains = jnp.concatenate([sums_down[2], sums_up[2]], axis=0)
        return grad_w_in, grad_w_out, grad_gains, loss_value.reshape(1)

    block_spec = P(('dp', 'stage'))
    return jax.shard_map(device_step, mesh=mesh,
                         in_specs=(P('dp'), P('dp'), P('stage'), P('stage'), P('stage')),
                         out_specs=(block_spec, block_spec, block_spec, P('dp')),
                         check_vma=False)
```

profile of v0, /device:TPU:112, one launch (start us, length us, event | category | flops | bytes accessed | tf_op | source)
XLA Modules:
  0.0 3301.7 jit_solution(5113446543467133171)
XLA Ops:
  39.1 1011.9 %while.47 = (s32[]{:T(128)}, bf16[512,1024]{1,0:T(8,128)(2,1)}, bf16[512,1024]{1,0:T(8,128)(2,1)S(1)}, bf16[1,8,512,1024]{3,2,1,0:T(8,128)(2,1)}, bf16[1,8,512,1...) while((s32[]{:T(128)}, bf16[512,1024]{1,0:T(8,128)(2,1)}, ...), condition=%wide.region_7.8_spmd.clone, body=%wide.region_0.7_spmd.clone.sunk | while | flops 17231249408 | bytes 72376864 | solution.py:119
  361.0 21.0 collective-permute-start
  467.1 16.6 collective-permute-start
  503.2 24.8 collective-permute-start
  547.5 50.5 %collective-permute-start = (bf16[512,1024]{1,0:T(8,128)(2,1)}, bf16[512,1024]{1,0:T(8,128)(2,1)}, u32[]{:S(2)}, u32[]{:S(2)}) collective-permute-start(bf16[512,1024]{1,0:T(8,128)(2,1)} %get-tuple-element.942), channel_id=1, source_target_pairs={{0,1},{1,2},{2,3},{3,4},{4,5},{5,6},{6,7},{8,9},{9,10},{10,11},{11... | collective-permute-start | bytes 3145736 | tf_op jit(solution)/shard_map/while/body/eval_jaxpr/ppermute | solution.py:113
  617.4 50.9 %collective-permute-start = (bf16[512,1024]{1,0:T(8,128)(2,1)}, bf16[512,1024]{1,0:T(8,128)(2,1)}, u32[]{:S(2)}, u32[]{:S(2)}) collective-permute-start(bf16[512,1024]{1,0:T(8,128)(2,1)} %get-tuple-element.942), channel_id=1, source_target_pairs={{0,1},{1,2},{2,3},{3,4},{4,5},{5,6},{6,7},{8,9},{9,10},{10,11},{11... | collective-permute-start | bytes 3145736 | tf_op jit(solution)/shard_map/while/body/eval_jaxpr/ppermute | solution.py:113
  744.4 20.4 collective-permute-start
  1110.1 2146.9 %while.48 = (s32[]{:T(128)}, bf16[512,1024]{1,0:T(8,128)(2,1)}, bf16[512,1024]{1,0:T(8,128)(2,1)S(1)}, f32[1,1024,4096]{2,1,0:T(8,128)}, f32[1,4096,1024]{2,1,0:...) while((s32[]{:T(128)}, bf16[512,1024]{1,0:T(8,128)(2,1)}, ...), condition=%wide.region_19.20_spmd.clone, body=%wide.region_8.19_spmd.clone.sunk | while | flops 43119017984 | bytes 310494016 | solution.py:161
  1137.0 58.0 %conditional.14 = (bf16[512,1024]{1,0:T(8,128)(2,1)}, f32[1,1024,4096]{2,1,0:T(8,128)}, f32[1,4096,1024]{2,1,0:T(8,128)}, f32[1,1024]{1,0:T(1,128)S(1)}) conditional(s32[]{:T(128)} %convert_element_type.316, (f32[1,1024,4096]{2,1,0:T(8,128)}, f32[1,4096,1024]{2,1,0:T(8,128)}, f32[1,1024]{1,0:T(1,128)S(1)}) %tuple.109, (pred[]{:T(512)}, s32[]{:T(128)}, ...), branch_computations={%region_9.9_spmd, %region_10.13_spmd} | conditional | flops 21558722560 | bytes 146858064 | solution.py:149
  1204.2 58.0 %conditional.14 = (bf16[512,1024]{1,0:T(8,128)(2,1)}, f32[1,1024,4096]{2,1,0:T(8,128)}, f32[1,4096,1024]{2,1,0:T(8,128)}, f32[1,1024]{1,0:T(1,128)S(1)}) conditional(s32[]{:T(128)} %convert_element_type.316, (f32[1,1024,4096]{2,1,0:T(8,128)}, f32[1,4096,1024]{2,1,0:T(8,128)}, f32[1,1024]{1,0:T(1,128)S(1)}) %tuple.109, (pred[]{:T(512)}, s32[]{:T(128)}, ...), branch_computations={%region_9.9_spmd, %region_10.13_spmd} | conditional | flops 21558722560 | bytes 146858064 | solution.py:149
  1273.5 58.0 %conditional.14 = (bf16[512,1024]{1,0:T(8,128)(2,1)}, f32[1,1024,4096]{2,1,0:T(8,128)}, f32[1,4096,1024]{2,1,0:T(8,128)}, f32[1,1024]{1,0:T(1,128)S(1)}) conditional(s32[]{:T(128)} %convert_element_type.316, (f32[1,1024,4096]{2,1,0:T(8,128)}, f32[1,4096,1024]{2,1,0:T(8,128)}, f32[1,1024]{1,0:T(1,128)S(1)}) %tuple.109, (pred[]{:T(512)}, s32[]{:T(128)}, ...), branch_computations={%region_9.9_spmd, %region_10.13_spmd} | conditional | flops 21558722560 | bytes 146858064 | solution.py:149
  1351.6 58.0 %conditional.14 = (bf16[512,1024]{1,0:T(8,128)(2,1)}, f32[1,1024,4096]{2,1,0:T(8,128)}, f32[1,4096,1024]{2,1,0:T(8,128)}, f32[1,1024]{1,0:T(1,128)S(1)}) conditional(s32[]{:T(128)} %convert_element_type.316, (f32[1,1024,4096]{2,1,0:T(8,128)}, f32[1,4096,1024]{2,1,0:T(8,128)}, f32[1,1024]{1,0:T(1,128)S(1)}) %tuple.109, (pred[]{:T(512)}, s32[]{:T(128)}, ...), branch_computations={%region_9.9_spmd, %region_10.13_spmd} | conditional | flops 21558722560 | bytes 146858064 | solution.py:149
  1432.2 58.0 %conditional.14 = (bf16[512,1024]{1,0:T(8,128)(2,1)}, f32[1,1024,4096]{2,1,0:T(8,128)}, f32[1,4096,1024]{2,1,0:T(8,128)}, f32[1,1024]{1,0:T(1,128)S(1)}) conditional(s32[]{:T(128)} %convert_element_type.316, (f32[1,1024,4096]{2,1,0:T(8,128)}, f32[1,4096,1024]{2,1,0:T(8,128)}, f32[1,1024]{1,0:T(1,128)S(1)}) %tuple.109, (pred[]{:T(512)}, s32[]{:T(128)}, ...), branch_computations={%region_9.9_spmd, %region_10.13_spmd} | conditional | flops 21558722560 | bytes 146858064 | solution.py:149
  1512.8 58.0 %conditional.14 = (bf16[512,1024]{1,0:T(8,128)(2,1)}, f32[1,1024,4096]{2,1,0:T(8,128)}, f32[1,4096,1024]{2,1,0:T(8,128)}, f32[1,1024]{1,0:T(1,128)S(1)}) conditional(s32[]{:T(128)} %convert_element_type.316, (f32[1,1024,4096]{2,1,0:T(8,128)}, f32[1,4096,1024]{2,1,0:T(8,128)}, f32[1,1024]{1,0:T(1,128)S(1)}) %tuple.109, (pred[]{:T(512)}, s32[]{:T(128)}, ...), branch_computations={%region_9.9_spmd, %region_10.13_spmd} | conditional | flops 21558722560 | bytes 146858064 | solution.py:149
  1593.4 58.0 %conditional.14 = (bf16[512,1024]{1,0:T(8,128)(2,1)}, f32[1,1024,4096]{2,1,0:T(8,128)}, f32[1,4096,1024]{2,1,0:T(8,128)}, f32[1,1024]{1,0:T(1,128)S(1)}) conditional(s32[]{:T(128)} %convert_element_type.316, (f32[1,1024,4096]{2,1,0:T(8,128)}, f32[1,4096,1024]{2,1,0:T(8,128)}, f32[1,1024]{1,0:T(1,128)S(1)}) %tuple.109, (pred[]{:T(512)}, s32[]{:T(128)}, ...), branch_computations={%region_9.9_spmd, %region_10.13_spmd} | conditional | flops 21558722560 | bytes 146858064 | solution.py:149
  1674.0 58.0 %conditional.14 = (bf16[512,1024]{1,0:T(8,128)(2,1)}, f32[1,1024,4096]{2,1,0:T(8,128)}, f32[1,4096,1024]{2,1,0:T(8,128)}, f32[1,1024]{1,0:T(1,128)S(1)}) conditional(s32[]{:T(128)} %convert_element_type.316, (f32[1,1024,4096]{2,1,0:T(8,128)}, f32[1,4096,1024]{2,1,0:T(8,128)}, f32[1,1024]{1,0:T(1,128)S(1)}) %tuple.109, (pred[]{:T(512)}, s32[]{:T(128)}, ...), branch_computations={%region_9.9_spmd, %region_10.13_spmd} | conditional | flops 21558722560 | bytes 146858064 | solution.py:149
  1755.7 71.7 %collective-permute-start.2 = (bf16[512,1024]{1,0:T(8,128)(2,1)}, bf16[512,1024]{1,0:T(8,128)(2,1)S(1)}, u32[]{:S(2)}, u32[]{:S(2)}) collective-permute-start(bf16[512,1024]{1,0:T(8,128)(2,1)} %get-tuple-element.971), channel_id=1, source_target_pairs={{0,1},{1,2},{2,3},{3,4},{4,5},{5,6},{6,7},{8,9},{9,10},{10,11},{11... | collective-permute-start | bytes 3145736 | tf_op jit(solution)/shard_map/while/body/eval_jaxpr/ppermute | solution.py:152
  1859.6 71.7 %collective-permute-start.2 = (bf16[512,1024]{1,0:T(8,128)(2,1)}, bf16[512,1024]{1,0:T(8,128)(2,1)S(1)}, u32[]{:S(2)}, u32[]{:S(2)}) collective-permute-start(bf16[512,1024]{1,0:T(8,128)(2,1)} %get-tuple-element.971), channel_id=1, source_target_pairs={{0,1},{1,2},{2,3},{3,4},{4,5},{5,6},{6,7},{8,9},{9,10},{10,11},{11... | collective-permute-start | bytes 3145736 | tf_op jit(solution)/shard_map/while/body/eval_jaxpr/ppermute | solution.py:152
  1963.6 60.3 %collective-permute-start.2 = (bf16[512,1024]{1,0:T(8,128)(2,1)}, bf16[512,1024]{1,0:T(8,128)(2,1)S(1)}, u32[]{:S(2)}, u32[]{:S(2)}) collective-permute-start(bf16[512,1024]{1,0:T(8,128)(2,1)} %get-tuple-element.971), channel_id=1, source_target_pairs={{0,1},{1,2},{2,3},{3,4},{4,5},{5,6},{6,7},{8,9},{9,10},{10,11},{11... | collective-permute-start | bytes 3145736 | tf_op jit(solution)/shard_map/while/body/eval_jaxpr/ppermute | solution.py:152
  2056.2 419.1 %collective-permute-start.2 = (bf16[512,1024]{1,0:T(8,128)(2,1)}, bf16[512,1024]{1,0:T(8,128)(2,1)S(1)}, u32[]{:S(2)}, u32[]{:S(2)}) collective-permute-start(bf16[512,1024]{1,0:T(8,128)(2,1)} %get-tuple-element.971), channel_id=1, source_target_pairs={{0,1},{1,2},{2,3},{3,4},{4,5},{5,6},{6,7},{8,9},{9,10},{10,11},{11... | collective-permute-start | bytes 3145736 | tf_op jit(solution)/shard_map/while/body/eval_jaxpr/ppermute | solution.py:152
  2479.9 56.5 %conditional.15 = (bf16[512,1024]{1,0:T(8,128)(2,1)}, f32[1,1024,4096]{2,1,0:T(8,128)}, f32[1,4096,1024]{2,1,0:T(8,128)}, f32[1,1024]{1,0:T(1,128)S(1)}) conditional(s32[]{:T(128)} %convert_element_type.317, (f32[1,1024,4096]{2,1,0:T(8,128)}, f32[1,4096,1024]{2,1,0:T(8,128)}, f32[1,1024]{1,0:T(1,128)S(1)}) %tuple.111, (s32[]{:T(128)}, ...), branch_computations={%region_14.14_spmd, %region_15.18_spmd.clone} | conditional | flops 21559771136 | bytes 143712336 | solution.py:150
  2558.6 56.5 %conditional.15 = (bf16[512,1024]{1,0:T(8,128)(2,1)}, f32[1,1024,4096]{2,1,0:T(8,128)}, f32[1,4096,1024]{2,1,0:T(8,128)}, f32[1,1024]{1,0:T(1,128)S(1)}) conditional(s32[]{:T(128)} %convert_element_type.317, (f32[1,1024,4096]{2,1,0:T(8,128)}, f32[1,4096,1024]{2,1,0:T(8,128)}, f32[1,1024]{1,0:T(1,128)S(1)}) %tuple.111, (s32[]{:T(128)}, ...), branch_computations={%region_14.14_spmd, %region_15.18_spmd.clone} | conditional | flops 21559771136 | bytes 143712336 | solution.py:150
  2618.2 71.7 %collective-permute-start.2 = (bf16[512,1024]{1,0:T(8,128)(2,1)}, bf16[512,1024]{1,0:T(8,128)(2,1)S(1)}, u32[]{:S(2)}, u32[]{:S(2)}) collective-permute-start(bf16[512,1024]{1,0:T(8,128)(2,1)} %get-tuple-element.971), channel_id=1, source_target_pairs={{0,1},{1,2},{2,3},{3,4},{4,5},{5,6},{6,7},{8,9},{9,10},{10,11},{11... | collective-permute-start | bytes 3145736 | tf_op jit(solution)/shard_map/while/body/eval_jaxpr/ppermute | solution.py:152
  2694.5 56.5 %conditional.15 = (bf16[512,1024]{1,0:T(8,128)(2,1)}, f32[1,1024,4096]{2,1,0:T(8,128)}, f32[1,4096,1024]{2,1,0:T(8,128)}, f32[1,1024]{1,0:T(1,128)S(1)}) conditional(s32[]{:T(128)} %convert_element_type.317, (f32[1,1024,4096]{2,1,0:T(8,128)}, f32[1,4096,1024]{2,1,0:T(8,128)}, f32[1,1024]{1,0:T(1,128)S(1)}) %tuple.111, (s32[]{:T(128)}, ...), branch_computations={%region_14.14_spmd, %region_15.18_spmd.clone} | conditional | flops 21559771136 | bytes 143712336 | solution.py:150
  2773.2 56.5 %conditional.15 = (bf16[512,1024]{1,0:T(8,128)(2,1)}, f32[1,1024,4096]{2,1,0:T(8,128)}, f32[1,4096,1024]{2,1,0:T(8,128)}, f32[1,1024]{1,0:T(1,128)S(1)}) conditional(s32[]{:T(128)} %convert_element_type.317, (f32[1,1024,4096]{2,1,0:T(8,128)}, f32[1,4096,1024]{2,1,0:T(8,128)}, f32[1,1024]{1,0:T(1,128)S(1)}) %tuple.111, (s32[]{:T(128)}, ...), branch_computations={%region_14.14_spmd, %region_15.18_spmd.clone} | conditional | flops 21559771136 | bytes 143712336 | solution.py:150
  2832.8 71.7 %collective-permute-start.2 = (bf16[512,1024]{1,0:T(8,128)(2,1)}, bf16[512,1024]{1,0:T(8,128)(2,1)S(1)}, u32[]{:S(2)}, u32[]{:S(2)}) collective-permute-start(bf16[512,1024]{1,0:T(8,128)(2,1)} %get-tuple-element.971), channel_id=1, source_target_pairs={{0,1},{1,2},{2,3},{3,4},{4,5},{5,6},{6,7},{8,9},{9,10},{10,11},{11... | collective-permute-start | bytes 3145736 | tf_op jit(solution)/shard_map/while/body/eval_jaxpr/ppermute | solution.py:152
  2909.1 56.5 %conditional.15 = (bf16[512,1024]{1,0:T(8,128)(2,1)}, f32[1,1024,4096]{2,1,0:T(8,128)}, f32[1,4096,1024]{2,1,0:T(8,128)}, f32[1,1024]{1,0:T(1,128)S(1)}) conditional(s32[]{:T(128)} %convert_element_type.317, (f32[1,1024,4096]{2,1,0:T(8,128)}, f32[1,4096,1024]{2,1,0:T(8,128)}, f32[1,1024]{1,0:T(1,128)S(1)}) %tuple.111, (s32[]{:T(128)}, ...), branch_computations={%region_14.14_spmd, %region_15.18_spmd.clone} | conditional | flops 21559771136 | bytes 143712336 | solution.py:150
  2987.8 56.5 %conditional.15 = (bf16[512,1024]{1,0:T(8,128)(2,1)}, f32[1,1024,4096]{2,1,0:T(8,128)}, f32[1,4096,1024]{2,1,0:T(8,128)}, f32[1,1024]{1,0:T(1,128)S(1)}) conditional(s32[]{:T(128)} %convert_element_type.317, (f32[1,1024,4096]{2,1,0:T(8,128)}, f32[1,4096,1024]{2,1,0:T(8,128)}, f32[1,1024]{1,0:T(1,128)S(1)}) %tuple.111, (s32[]{:T(128)}, ...), branch_computations={%region_14.14_spmd, %region_15.18_spmd.clone} | conditional | flops 21559771136 | bytes 143712336 | solution.py:150
  3047.4 60.3 %collective-permute-start.2 = (bf16[512,1024]{1,0:T(8,128)(2,1)}, bf16[512,1024]{1,0:T(8,128)(2,1)S(1)}, u32[]{:S(2)}, u32[]{:S(2)}) collective-permute-start(bf16[512,1024]{1,0:T(8,128)(2,1)} %get-tuple-element.971), channel_id=1, source_target_pairs={{0,1},{1,2},{2,3},{3,4},{4,5},{5,6},{6,7},{8,9},{9,10},{10,11},{11... | collective-permute-start | bytes 3145736 | tf_op jit(solution)/shard_map/while/body/eval_jaxpr/ppermute | solution.py:152
  3112.3 56.5 %conditional.15 = (bf16[512,1024]{1,0:T(8,128)(2,1)}, f32[1,1024,4096]{2,1,0:T(8,128)}, f32[1,4096,1024]{2,1,0:T(8,128)}, f32[1,1024]{1,0:T(1,128)S(1)}) conditional(s32[]{:T(128)} %convert_element_type.317, (f32[1,1024,4096]{2,1,0:T(8,128)}, f32[1,4096,1024]{2,1,0:T(8,128)}, f32[1,1024]{1,0:T(1,128)S(1)}) %tuple.111, (s32[]{:T(128)}, ...), branch_computations={%region_14.14_spmd, %region_15.18_spmd.clone} | conditional | flops 21559771136 | bytes 143712336 | solution.py:150
  3191.0 56.5 %conditional.15 = (bf16[512,1024]{1,0:T(8,128)(2,1)}, f32[1,1024,4096]{2,1,0:T(8,128)}, f32[1,4096,1024]{2,1,0:T(8,128)}, f32[1,1024]{1,0:T(1,128)S(1)}) conditional(s32[]{:T(128)} %convert_element_type.317, (f32[1,1024,4096]{2,1,0:T(8,128)}, f32[1,4096,1024]{2,1,0:T(8,128)}, f32[1,1024]{1,0:T(1,128)S(1)}) %tuple.111, (s32[]{:T(128)}, ...), branch_computations={%region_14.14_spmd, %region_15.18_spmd.clone} | conditional | flops 21559771136 | bytes 143712336 | solution.py:150
  3257.0 26.7 pad_maximum_fusion
  (930 shorter events, 2497.0 us)
Async XLA Ops:
  361.0 36.6 %collective-permute-start = (bf16[512,1024]{1,0:T(8,128)(2,1)}, bf16[512,1024]{1,0:T(8,128)(2,1)}, u32[]{:S(2)}, u32[]{:S(2)}) collective-permute-start(bf16[512,1024]{1,0:T(8,128)(2,1)} %get-tuple-element.942), channel_id=1, source_target_pairs={{0,1},{1,2},{2,3},{3,4},{4,5},{5,6},{6,7},{8,9},{9,10},{10,11},{11... | collective-permute-start | bytes 3145736 | tf_op jit(solution)/shard_map/while/body/eval_jaxpr/ppermute | solution.py:113
  503.2 40.5 %collective-permute-start = (bf16[512,1024]{1,0:T(8,128)(2,1)}, bf16[512,1024]{1,0:T(8,128)(2,1)}, u32[]{:S(2)}, u32[]{:S(2)}) collective-permute-start(bf16[512,1024]{1,0:T(8,128)(2,1)} %get-tuple-element.942), channel_id=1, source_target_pairs={{0,1},{1,2},{2,3},{3,4},{4,5},{5,6},{6,7},{8,9},{9,10},{10,11},{11... | collective-permute-start | bytes 3145736 | tf_op jit(solution)/shard_map/while/body/eval_jaxpr/ppermute | solution.py:113
  547.5 66.2 %collective-permute-start = (bf16[512,1024]{1,0:T(8,128)(2,1)}, bf16[512,1024]{1,0:T(8,128)(2,1)}, u32[]{:S(2)}, u32[]{:S(2)}) collective-permute-start(bf16[512,1024]{1,0:T(8,128)(2,1)} %get-tuple-element.942), channel_id=1, source_target_pairs={{0,1},{1,2},{2,3},{3,4},{4,5},{5,6},{6,7},{8,9},{9,10},{10,11},{11... | collective-permute-start | bytes 3145736 | tf_op jit(solution)/shard_map/while/body/eval_jaxpr/ppermute | solution.py:113
  617.4 72.2 %collective-permute-start = (bf16[512,1024]{1,0:T(8,128)(2,1)}, bf16[512,1024]{1,0:T(8,128)(2,1)}, u32[]{:S(2)}, u32[]{:S(2)}) collective-permute-start(bf16[512,1024]{1,0:T(8,128)(2,1)} %get-tuple-element.942), channel_id=1, source_target_pairs={{0,1},{1,2},{2,3},{3,4},{4,5},{5,6},{6,7},{8,9},{9,10},{10,11},{11... | collective-permute-start | bytes 3145736 | tf_op jit(solution)/shard_map/while/body/eval_jaxpr/ppermute | solution.py:113
  693.4 47.2 %collective-permute-start = (bf16[512,1024]{1,0:T(8,128)(2,1)}, bf16[512,1024]{1,0:T(8,128)(2,1)}, u32[]{:S(2)}, u32[]{:S(2)}) collective-permute-start(bf16[512,1024]{1,0:T(8,128)(2,1)} %get-tuple-element.942), channel_id=1, source_target_pairs={{0,1},{1,2},{2,3},{3,4},{4,5},{5,6},{6,7},{8,9},{9,10},{10,11},{11... | collective-permute-start | bytes 3145736 | tf_op jit(solution)/shard_map/while/body/eval_jaxpr/ppermute | solution.py:113
  744.4 52.2 %collective-permute-start = (bf16[512,1024]{1,0:T(8,128)(2,1)}, bf16[512,1024]{1,0:T(8,128)(2,1)}, u32[]{:S(2)}, u32[]{:S(2)}) collective-permute-start(bf16[512,1024]{1,0:T(8,128)(2,1)} %get-tuple-element.942), channel_id=1, source_target_pairs={{0,1},{1,2},{2,3},{3,4},{4,5},{5,6},{6,7},{8,9},{9,10},{10,11},{11... | collective-permute-start | bytes 3145736 | tf_op jit(solution)/shard_map/while/body/eval_jaxpr/ppermute | solution.py:113
  800.3 48.2 %collective-permute-start = (bf16[512,1024]{1,0:T(8,128)(2,1)}, bf16[512,1024]{1,0:T(8,128)(2,1)}, u32[]{:S(2)}, u32[]{:S(2)}) collective-permute-start(bf16[512,1024]{1,0:T(8,128)(2,1)} %get-tuple-element.942), channel_id=1, source_target_pairs={{0,1},{1,2},{2,3},{3,4},{4,5},{5,6},{6,7},{8,9},{9,10},{10,11},{11... | collective-permute-start | bytes 3145736 | tf_op jit(solution)/shard_map/while/body/eval_jaxpr/ppermute | solution.py:113
  852.3 36.6 %collective-permute-start = (bf16[512,1024]{1,0:T(8,128)(2,1)}, bf16[512,1024]{1,0:T(8,128)(2,1)}, u32[]{:S(2)}, u32[]{:S(2)}) collective-permute-start(bf16[512,1024]{1,0:T(8,128)(2,1)} %get-tuple-element.942), channel_id=1, source_target_pairs={{0,1},{1,2},{2,3},{3,4},{4,5},{5,6},{6,7},{8,9},{9,10},{10,11},{11... | collective-permute-start | bytes 3145736 | tf_op jit(solution)/shard_map/while/body/eval_jaxpr/ppermute | solution.py:113
  892.8 36.6 %collective-permute-start = (bf16[512,1024]{1,0:T(8,128)(2,1)}, bf16[512,1024]{1,0:T(8,128)(2,1)}, u32[]{:S(2)}, u32[]{:S(2)}) collective-permute-start(bf16[512,1024]{1,0:T(8,128)(2,1)} %get-tuple-element.942), channel_id=1, source_target_pairs={{0,1},{1,2},{2,3},{3,4},{4,5},{5,6},{6,7},{8,9},{9,10},{10,11},{11... | collective-permute-start | bytes 3145736 | tf_op jit(solution)/shard_map/while/body/eval_jaxpr/ppermute | solution.py:113
  933.2 36.6 %collective-permute-start = (bf16[512,1024]{1,0:T(8,128)(2,1)}, bf16[512,1024]{1,0:T(8,128)(2,1)}, u32[]{:S(2)}, u32[]{:S(2)}) collective-permute-start(bf16[512,1024]{1,0:T(8,128)(2,1)} %get-tuple-element.942), channel_id=1, source_target_pairs={{0,1},{1,2},{2,3},{3,4},{4,5},{5,6},{6,7},{8,9},{9,10},{10,11},{11... | collective-permute-start | bytes 3145736 | tf_op jit(solution)/shard_map/while/body/eval_jaxpr/ppermute | solution.py:113
  1135.0 61.4 %collective-permute-start.3 = (bf16[512,1024]{1,0:T(8,128)(2,1)}, bf16[512,1024]{1,0:T(8,128)(2,1)S(1)}, u32[]{:S(2)}, u32[]{:S(2)}) collective-permute-start(bf16[512,1024]{1,0:T(8,128)(2,1)} %get-tuple-element.972), channel_id=1, source_target_pairs={{1,0},{2,1},{3,2},{4,3},{5,4},{6,5},{7,6},{9,8},{10,9},{11,10},{12... | collective-permute-start | bytes 3145736 | tf_op jit(solution)/shard_map/while/body/eval_jaxpr/ppermute | solution.py:153
  1202.2 63.5 %collective-permute-start.3 = (bf16[512,1024]{1,0:T(8,128)(2,1)}, bf16[512,1024]{1,0:T(8,128)(2,1)S(1)}, u32[]{:S(2)}, u32[]{:S(2)}) collective-permute-start(bf16[512,1024]{1,0:T(8,128)(2,1)} %get-tuple-element.972), channel_id=1, source_target_pairs={{1,0},{2,1},{3,2},{4,3},{5,4},{6,5},{7,6},{9,8},{10,9},{11,10},{12... | collective-permute-start | bytes 3145736 | tf_op jit(solution)/shard_map/while/body/eval_jaxpr/ppermute | solution.py:153
  1271.5 72.3 %collective-permute-start.3 = (bf16[512,1024]{1,0:T(8,128)(2,1)}, bf16[512,1024]{1,0:T(8,128)(2,1)S(1)}, u32[]{:S(2)}, u32[]{:S(2)}) collective-permute-start(bf16[512,1024]{1,0:T(8,128)(2,1)} %get-tuple-element.972), channel_id=1, source_target_pairs={{1,0},{2,1},{3,2},{4,3},{5,4},{6,5},{7,6},{9,8},{10,9},{11,10},{12... | collective-permute-start | bytes 3145736 | tf_op jit(solution)/shard_map/while/body/eval_jaxpr/ppermute | solution.py:153
  1349.6 74.8 %collective-permute-start.3 = (bf16[512,1024]{1,0:T(8,128)(2,1)}, bf16[512,1024]{1,0:T(8,128)(2,1)S(1)}, u32[]{:S(2)}, u32[]{:S(2)}) collective-permute-start(bf16[512,1024]{1,0:T(8,128)(2,1)} %get-tuple-element.972), channel_id=1, source_target_pairs={{1,0},{2,1},{3,2},{4,3},{5,4},{6,5},{7,6},{9,8},{10,9},{11,10},{12... | collective-permute-start | bytes 3145736 | tf_op jit(solution)/shard_map/while/body/eval_jaxpr/ppermute | solution.py:153
  1430.2 74.8 %collective-permute-start.3 = (bf16[512,1024]{1,0:T(8,128)(2,1)}, bf16[512,1024]{1,0:T(8,128)(2,1)S(1)}, u32[]{:S(2)}, u32[]{:S(2)}) collective-permute-start(bf16[512,1024]{1,0:T(8,128)(2,1)} %get-tuple-element.972), channel_id=1, source_target_pairs={{1,0},{2,1},{3,2},{4,3},{5,4},{6,5},{7,6},{9,8},{10,9},{11,10},{12... | collective-permute-start | bytes 3145736 | tf_op jit(solution)/shard_map/while/body/eval_jaxpr/ppermute | solution.py:153
  1510.8 74.8 %collective-permute-start.3 = (bf16[512,1024]{1,0:T(8,128)(2,1)}, bf16[512,1024]{1,0:T(8,128)(2,1)S(1)}, u32[]{:S(2)}, u32[]{:S(2)}) collective-permute-start(bf16[512,1024]{1,0:T(8,128)(2,1)} %get-tuple-element.972), channel_id=1, source_target_pairs={{1,0},{2,1},{3,2},{4,3},{5,4},{6,5},{7,6},{9,8},{10,9},{11,10},{12... | collective-permute-start | bytes 3145736 | tf_op jit(solution)/shard_map/while/body/eval_jaxpr/ppermute | solution.py:153
  1591.4 74.8 %collective-permute-start.3 = (bf16[512,1024]{1,0:T(8,128)(2,1)}, bf16[512,1024]{1,0:T(8,128)(2,1)S(1)}, u32[]{:S(2)}, u32[]{:S(2)}) collective-permute-start(bf16[512,1024]{1,0:T(8,128)(2,1)} %get-tuple-element.972), channel_id=1, source_target_pairs={{1,0},{2,1},{3,2},{4,3},{5,4},{6,5},{7,6},{9,8},{10,9},{11,10},{12... | collective-permute-start | bytes 3145736 | tf_op jit(solution)/shard_map/while/body/eval_jaxpr/ppermute | solution.py:153
  1672.0 74.8 %collective-permute-start.3 = (bf16[512,1024]{1,0:T(8,128)(2,1)}, bf16[512,1024]{1,0:T(8,128)(2,1)S(1)}, u32[]{:S(2)}, u32[]{:S(2)}) collective-permute-start(bf16[512,1024]{1,0:T(8,128)(2,1)} %get-tuple-element.972), channel_id=1, source_target_pairs={{1,0},{2,1},{3,2},{4,3},{5,4},{6,5},{7,6},{9,8},{10,9},{11,10},{12... | collective-permute-start | bytes 3145736 | tf_op jit(solution)/shard_map/while/body/eval_jaxpr/ppermute | solution.py:153
  1752.6 74.8 %collective-permute-start.3 = (bf16[512,1024]{1,0:T(8,128)(2,1)}, bf16[512,1024]{1,0:T(8,128)(2,1)S(1)}, u32[]{:S(2)}, u32[]{:S(2)}) collective-permute-start(bf16[512,1024]{1,0:T(8,128)(2,1)} %get-tuple-element.972), channel_id=1, source_target_pairs={{1,0},{2,1},{3,2},{4,3},{5,4},{6,5},{7,6},{9,8},{10,9},{11,10},{12... | collective-permute-start | bytes 3145736 | tf_op jit(solution)/shard_map/while/body/eval_jaxpr/ppermute | solution.py:153
  1755.7 74.0 %collective-permute-start.2 = (bf16[512,1024]{1,0:T(8,128)(2,1)}, bf16[512,1024]{1,0:T(8,128)(2,1)S(1)}, u32[]{:S(2)}, u32[]{:S(2)}) collective-permute-start(bf16[512,1024]{1,0:T(8,128)(2,1)} %get-tuple-element.971), channel_id=1, source_target_pairs={{0,1},{1,2},{2,3},{3,4},{4,5},{5,6},{6,7},{8,9},{9,10},{10,11},{11... | collective-permute-start | bytes 3145736 | tf_op jit(solution)/shard_map/while/body/eval_jaxpr/ppermute | solution.py:152
  1856.5 74.8 %collective-permute-start.3 = (bf16[512,1024]{1,0:T(8,128)(2,1)}, bf16[512,1024]{1,0:T(8,128)(2,1)S(1)}, u32[]{:S(2)}, u32[]{:S(2)}) collective-permute-start(bf16[512,1024]{1,0:T(8,128)(2,1)} %get-tuple-element.972), channel_id=1, source_target_pairs={{1,0},{2,1},{3,2},{4,3},{5,4},{6,5},{7,6},{9,8},{10,9},{11,10},{12... | collective-permute-start | bytes 3145736 | tf_op jit(solution)/shard_map/while/body/eval_jaxpr/ppermute | solution.py:153
  1859.6 74.0 %collective-permute-start.2 = (bf16[512,1024]{1,0:T(8,128)(2,1)}, bf16[512,1024]{1,0:T(8,128)(2,1)S(1)}, u32[]{:S(2)}, u32[]{:S(2)}) collective-permute-start(bf16[512,1024]{1,0:T(8,128)(2,1)} %get-tuple-element.971), channel_id=1, source_target_pairs={{0,1},{1,2},{2,3},{3,4},{4,5},{5,6},{6,7},{8,9},{9,10},{10,11},{11... | collective-permute-start | bytes 3145736 | tf_op jit(solution)/shard_map/while/body/eval_jaxpr/ppermute | solution.py:152
  1960.5 63.4 %collective-permute-start.3 = (bf16[512,1024]{1,0:T(8,128)(2,1)}, bf16[512,1024]{1,0:T(8,128)(2,1)S(1)}, u32[]{:S(2)}, u32[]{:S(2)}) collective-permute-start(bf16[512,1024]{1,0:T(8,128)(2,1)} %get-tuple-element.972), channel_id=1, source_target_pairs={{1,0},{2,1},{3,2},{4,3},{5,4},{6,5},{7,6},{9,8},{10,9},{11,10},{12... | collective-permute-start | bytes 3145736 | tf_op jit(solution)/shard_map/while/body/eval_jaxpr/ppermute | solution.py:153
  1963.6 62.6 %collective-permute-start.2 = (bf16[512,1024]{1,0:T(8,128)(2,1)}, bf16[512,1024]{1,0:T(8,128)(2,1)S(1)}, u32[]{:S(2)}, u32[]{:S(2)}) collective-permute-start(bf16[512,1024]{1,0:T(8,128)(2,1)} %get-tuple-element.971), channel_id=1, source_target_pairs={{0,1},{1,2},{2,3},{3,4},{4,5},{5,6},{6,7},{8,9},{9,10},{10,11},{11... | collective-permute-start | bytes 3145736 | tf_op jit(solution)/shard_map/while/body/eval_jaxpr/ppermute | solution.py:152
  2053.1 422.3 %collective-permute-start.3 = (bf16[512,1024]{1,0:T(8,128)(2,1)}, bf16[512,1024]{1,0:T(8,128)(2,1)S(1)}, u32[]{:S(2)}, u32[]{:S(2)}) collective-permute-start(bf16[512,1024]{1,0:T(8,128)(2,1)} %get-tuple-element.972), channel_id=1, source_target_pairs={{1,0},{2,1},{3,2},{4,3},{5,4},{6,5},{7,6},{9,8},{10,9},{11,10},{12... | collective-permute-start | bytes 3145736 | tf_op jit(solution)/shard_map/while/body/eval_jaxpr/ppermute | solution.py:153
  2056.2 421.5 %collective-permute-start.2 = (bf16[512,1024]{1,0:T(8,128)(2,1)}, bf16[512,1024]{1,0:T(8,128)(2,1)S(1)}, u32[]{:S(2)}, u32[]{:S(2)}) collective-permute-start(bf16[512,1024]{1,0:T(8,128)(2,1)} %get-tuple-element.971), channel_id=1, source_target_pairs={{0,1},{1,2},{2,3},{3,4},{4,5},{5,6},{6,7},{8,9},{9,10},{10,11},{11... | collective-permute-start | bytes 3145736 | tf_op jit(solution)/shard_map/while/body/eval_jaxpr/ppermute | solution.py:152
  2615.1 74.8 %collective-permute-start.3 = (bf16[512,1024]{1,0:T(8,128)(2,1)}, bf16[512,1024]{1,0:T(8,128)(2,1)S(1)}, u32[]{:S(2)}, u32[]{:S(2)}) collective-permute-start(bf16[512,1024]{1,0:T(8,128)(2,1)} %get-tuple-element.972), channel_id=1, source_target_pairs={{1,0},{2,1},{3,2},{4,3},{5,4},{6,5},{7,6},{9,8},{10,9},{11,10},{12... | collective-permute-start | bytes 3145736 | tf_op jit(solution)/shard_map/while/body/eval_jaxpr/ppermute | solution.py:153
  2618.2 74.0 %collective-permute-start.2 = (bf16[512,1024]{1,0:T(8,128)(2,1)}, bf16[512,1024]{1,0:T(8,128)(2,1)S(1)}, u32[]{:S(2)}, u32[]{:S(2)}) collective-permute-start(bf16[512,1024]{1,0:T(8,128)(2,1)} %get-tuple-element.971), channel_id=1, source_target_pairs={{0,1},{1,2},{2,3},{3,4},{4,5},{5,6},{6,7},{8,9},{9,10},{10,11},{11... | collective-permute-start | bytes 3145736 | tf_op jit(solution)/shard_map/while/body/eval_jaxpr/ppermute | solution.py:152
  2829.7 74.8 %collective-permute-start.3 = (bf16[512,1024]{1,0:T(8,128)(2,1)}, bf16[512,1024]{1,0:T(8,128)(2,1)S(1)}, u32[]{:S(2)}, u32[]{:S(2)}) collective-permute-start(bf16[512,1024]{1,0:T(8,128)(2,1)} %get-tuple-element.972), channel_id=1, source_target_pairs={{1,0},{2,1},{3,2},{4,3},{5,4},{6,5},{7,6},{9,8},{10,9},{11,10},{12... | collective-permute-start | bytes 3145736 | tf_op jit(solution)/shard_map/while/body/eval_jaxpr/ppermute | solution.py:153
  2832.8 74.0 %collective-permute-start.2 = (bf16[512,1024]{1,0:T(8,128)(2,1)}, bf16[512,1024]{1,0:T(8,128)(2,1)S(1)}, u32[]{:S(2)}, u32[]{:S(2)}) collective-permute-start(bf16[512,1024]{1,0:T(8,128)(2,1)} %get-tuple-element.971), channel_id=1, source_target_pairs={{0,1},{1,2},{2,3},{3,4},{4,5},{5,6},{6,7},{8,9},{9,10},{10,11},{11... | collective-permute-start | bytes 3145736 | tf_op jit(solution)/shard_map/while/body/eval_jaxpr/ppermute | solution.py:152
  3044.3 63.4 %collective-permute-start.3 = (bf16[512,1024]{1,0:T(8,128)(2,1)}, bf16[512,1024]{1,0:T(8,128)(2,1)S(1)}, u32[]{:S(2)}, u32[]{:S(2)}) collective-permute-start(bf16[512,1024]{1,0:T(8,128)(2,1)} %get-tuple-element.972), channel_id=1, source_target_pairs={{1,0},{2,1},{3,2},{4,3},{5,4},{6,5},{7,6},{9,8},{10,9},{11,10},{12... | collective-permute-start | bytes 3145736 | tf_op jit(solution)/shard_map/while/body/eval_jaxpr/ppermute | solution.py:153
  3047.4 62.6 %collective-permute-start.2 = (bf16[512,1024]{1,0:T(8,128)(2,1)}, bf16[512,1024]{1,0:T(8,128)(2,1)S(1)}, u32[]{:S(2)}, u32[]{:S(2)}) collective-permute-start(bf16[512,1024]{1,0:T(8,128)(2,1)} %get-tuple-element.971), channel_id=1, source_target_pairs={{0,1},{1,2},{2,3},{3,4},{4,5},{5,6},{6,7},{8,9},{9,10},{10,11},{11... | collective-permute-start | bytes 3145736 | tf_op jit(solution)/shard_map/while/body/eval_jaxpr/ppermute | solution.py:152
  (111 other events, 1135.2 us)
where the time goes:
time: 3330 us; the launch traced here: 3300 us
  starting transfers between devices  1390 us (42%)
  matrix products  1090 us (33%)
  other arithmetic  360 us (11%)
  local copies, waits for them, and re-layouts  352 us (11%)
  loops' own time  90.2 us (3%)
    ppermute x23, starting transfers between devices, backward_tick(): recv_up = lax.ppermute(grad_up_out, 'stage', down_perm)  1020 us
    ppermute x23, starting transfers between devices, forward_tick(): recv_down = lax.ppermute(out_down, 'stage', down_perm)  304 us
    dot_general x16, matrix products, layer_forward(): out_f32 = jnp.dot(hidden, second_w, preferred_element_type=jnp.float32)  253 us
    dot_general x16, matrix products, layer_backward(): jnp.einsum('tf,td->fd', hidden, grad_h, preferred_element_type=jnp.float32)  206 us
    dot_general x16, matrix products, layer_backward(): jnp.einsum('td,tf->df', normed, grad_pre, preferred_element_type=jnp.floa...  194 us
    dot_general x16, matrix products, layer_backward(): jnp.einsum('td,fd->tf', grad_h, second_w, preferred_element_type=jnp.floa...  180 us
    dot_general x16, matrix products, layer_backward(): jnp.einsum('tf,df->td', grad_pre, first_w, preferred_element_type=jnp.flo...  136 us
    dot_general x16, matrix products, layer_backward(): pre_act = jnp.dot(normed, first_w, preferred_element_type=jnp.float32)  118 us
  transfers between devices with their start and end apart: 92, of which 2 were waited for; matrix products, arithmetic and copies ran while one was open for 29% of the time, Pallas kernels for 0%

commit v1 on v0

v1 whole, which is shorter than its diff:
```python
import functools

import jax
import jax.numpy as jnp
from jax import lax
from jax.experimental import pallas as pl
from jax.experimental.pallas import tpu as pltpu
from jax.sharding import PartitionSpec as P

EPSILON = 1e-6
GRAD_SLOTS = 4
GELU_C = 0.7978845608028654
GELU_A = 0.044715
F32 = jnp.float32
BF16 = jnp.bfloat16
NT = (((1,), (1,)), ((), ()))


def alpha_of(idx):
    return idx + lax.div(idx, 2)


def pipeline_kernel(stages, seed_scale, tokens, targets, w_in, w_out, gains,
                    u_st, da_st, n_st, dh_st, g_st, dgain, loss,
                    wi, wo, xf, bf, gbuf, ubuf, nbuf, obuf, dnbuf, tbuf, sse, sse_in,
                    fsem, bsem, osem, csem, wsem, gsem, usem, nsem, hsem, tsem, lsem, lsend):
    chunks, rows, d_model = tokens.shape
    d_ff = ubuf.shape[1]
    block = min(512, d_ff // 2)
    half = d_model // 2
    me = lax.axis_index('stage')
    last = stages - 1
    alpha = alpha_of(me)
    alpha_max = last + last // 2
    tick_count = 2 * alpha_max + 1 + 2 * (2 * chunks - 1) + 1

    def drain(ref, sem):
        pltpu.make_async_copy(ref, ref, sem).wait()

    barrier = pltpu.get_barrier_semaphore()
    for hop in range(1, stages):
        pl.semaphore_signal(barrier, inc=1, device_id={'stage': lax.rem(me + hop, stages)},
                            device_id_type=pl.DeviceIdType.MESH)
    pl.semaphore_wait(barrier, stages - 1)

    for row in range(2):
        pltpu.make_async_copy(w_in.at[row], wi.at[row], wsem.at[0, row]).start()
        pltpu.make_async_copy(w_out.at[row], wo.at[row], wsem.at[1, row]).start()

    @pl.when(me == 0)
    def _():
        def load_tokens(k, carry):
            pltpu.make_async_copy(tokens.at[k], xf.at[0, k], fsem.at[0, k]).start()
            return carry
        lax.fori_loop(0, chunks, load_tokens, 0)

    dgain[...] = jnp.zeros(dgain.shape, F32)
    sse[...] = jnp.zeros(sse.shape, F32)

    def decode(t):
        par = lax.rem(t + alpha, 2)
        base = alpha + par * (2 * alpha_max + 1 - 2 * alpha)
        step = lax.div(t - base + 8 * stages, 2) - 4 * stages
        return par, step

    def prefetch_slope(t):
        par, step = decode(t)

        @pl.when((step >= chunks) & (step < 2 * chunks))
        def _():
            pltpu.make_async_copy(g_st.at[1 - par, step - chunks], gbuf, gsem).start()

    def free_out(par, step):
        has_out = ((par == 0) & (me < last)) | ((par == 1) & ((me > 0) | (step <= chunks)))

        @pl.when((step > 0) & has_out)
        def _():
            drain(obuf.at[par], osem.at[par])

    def forward(t, par, k):
        x_ref = xf.at[par, k]
        sink = (par == 1) & (me == 0)
        turn = (par == 0) & (me == last)
        free_out(par, k)
        drain(x_ref, fsem.at[par, k])

        @pl.when(sink)
        def _():
            pltpu.make_async_copy(targets.at[k], tbuf, tsem).start()

        x_f32 = x_ref[...].astype(F32)
        inv_rms = lax.rsqrt(jnp.mean(x_f32 * x_f32, axis=-1, keepdims=True) + EPSILON)
        nbuf[...] = (x_f32 * inv_rms * gains[par]).astype(BF16)
        keep_n = pltpu.make_async_copy(nbuf, n_st.at[par, k], nsem)
        keep_n.start()

        @pl.when(k == 0)
        def _():
            drain(wi.at[par], wsem.at[0, par])

        for j in range(d_ff // block):
            cols = slice(j * block, (j + 1) * block)
            pre = jnp.dot(nbuf[...], wi[par, :, cols], preferred_element_type=F32)
            sq = pre * pre
            tanh = jnp.tanh(pre * (GELU_C + (GELU_C * GELU_A) * sq))
            cdf = 0.5 + 0.5 * tanh
            ubuf[:, cols] = (pre * cdf).astype(BF16)
            gbuf[:, cols] = cdf + pre * ((1.0 - tanh * tanh) * (0.5 * GELU_C + (1.5 * GELU_C * GELU_A) * sq))
        keep_u = pltpu.make_async_copy(ubuf, u_st.at[par, k], usem)
        keep_u.start()
        keep_g = pltpu.make_async_copy(gbuf, g_st.at[par, k], gsem)
        keep_g.start()

        @pl.when(k == 0)
        def _():
            drain(wo.at[par], wsem.at[1, par])

        for h in range(2):
            cols = slice(h * half, (h + 1) * half)
            out = x_ref[:, cols].astype(F32) + jnp.dot(ubuf[...], wo[par, :, cols], preferred_element_type=F32)
            obuf[par, :, cols] = out.astype(BF16)
            if h == 0:
                keep_g.wait()
                prefetch_slope(t + 1)

            @pl.when(turn)
            def _():
                pltpu.make_async_copy(obuf.at[0, :, cols], xf.at[1, k, :, cols], fsem.at[1, k]).start()

            @pl.when(jnp.logical_not(turn | sink))
            def _():
                pltpu.make_async_remote_copy(
                    src_ref=obuf.at[par, :, cols], dst_ref=xf.at[par, k, :, cols],
                    send_sem=osem.at[par], recv_sem=fsem.at[par, k],
                    device_id={'stage': me + 1 - 2 * par}, device_id_type=pl.DeviceIdType.MESH).start()

        @pl.when(sink)
        def _():
            drain(tbuf, tsem)
            error = obuf[1].astype(F32) - tbuf[...].astype(F32)
            sse[...] += jnp.sum((error * error).reshape(rows // 8, 8, d_model), axis=0)
            obuf[1] = (error * seed_scale).astype(BF16)
            pltpu.make_async_copy(obuf.at[1], dh_st.at[1, k], osem.at[1]).start()

            @pl.when(k == chunks - 1)
            def _():
                for hop in range(1, stages):
                    pltpu.make_async_remote_copy(
                        src_ref=sse, dst_ref=sse_in, send_sem=lsend.at[hop - 1], recv_sem=lsem,
                        device_id={'stage': hop}, device_id_type=pl.DeviceIdType.MESH).start()

        keep_n.wait()
        keep_u.wait()

    def backward(t, par, step):
        k = step - chunks
        row = 1 - par
        slot = lax.rem(k, GRAD_SLOTS)
        source = (par == 0) & (me == 0)
        sink = (par == 1) & (me == 0)
        turn = (par == 0) & (me == last)
        remote = jnp.logical_not(sink | turn)
        free_out(par, step)

        @pl.when(source & (k == 0))
        def _():
            pltpu.make_async_copy(dh_st.at[1, 0], bf.at[0, 0], bsem.at[0, 0]).start()

        @pl.when(source & (k < chunks - 1))
        def _():
            pltpu.make_async_copy(dh_st.at[1, k + 1], bf.at[0, lax.rem(k + 1, GRAD_SLOTS)],
                                  bsem.at[0, k + 1]).start()

        dh_ref = bf.at[par, slot]
        drain(dh_ref, bsem.at[par, k])
        keep_dh = pltpu.make_async_copy(dh_ref, dh_st.at[row, k], hsem)
        keep_dh.start()
        drain(gbuf, gsem)
        for j in range(d_ff // block):
            cols = slice(j * block, (j + 1) * block)
            d_hidden = lax.dot_general(dh_ref[...], wo[row, cols, :], NT, preferred_element_type=F32)
            ubuf[:, cols] = (d_hidden * gbuf[:, cols]).astype(BF16)
        prefetch_slope(t + 1)
        keep_da = pltpu.make_async_copy(ubuf, da_st.at[row, k], usem)
        keep_da.start()
        for h in range(2):
            cols = slice(h * half, (h + 1) * half)
            dnbuf[:, cols] = lax.dot_general(ubuf[...], wi[row, cols, :], NT, preferred_element_type=F32)
        x_f32 = xf[row, k].astype(F32)
        d_normed = dnbuf[...]
        inv_rms = lax.rsqrt(jnp.mean(x_f32 * x_f32, axis=-1, keepdims=True) + EPSILON)
        x_hat = x_f32 * inv_rms
        dgain[row] += jnp.sum((d_normed * x_hat).reshape(rows // 8, 8, d_model), axis=0)
        scaled = d_normed * gains[row]
        proj = jnp.mean(scaled * x_hat, axis=-1, keepdims=True)
        grad_x = dh_ref[...].astype(F32) + inv_rms * (scaled - x_hat * proj)
        obuf[par] = grad_x.astype(BF16)

        @pl.when(remote)
        def _():
            @pl.when(k >= GRAD_SLOTS)
            def _():
                pl.semaphore_wait(csem.at[par], 1)
            pltpu.make_async_remote_copy(
                src_ref=obuf.at[par], dst_ref=bf.at[par, slot],
                send_sem=osem.at[par], recv_sem=bsem.at[par, k],
                device_id={'stage': me + 1 - 2 * par}, device_id_type=pl.DeviceIdType.MESH).start()

        @pl.when(turn)
        def _():
            pltpu.make_async_copy(obuf.at[0], bf.at[1, slot], bsem.at[1, k]).start()

        keep_dh.wait()
        keep_da.wait()
        from_peer = ((par == 0) & (me > 0)) | ((par == 1) & (me < last))

        @pl.when(from_peer & (k < chunks - GRAD_SLOTS))
        def _():
            pl.semaphore_signal(csem.at[par], inc=1, device_id={'stage': me - 1 + 2 * par},
                                device_id_type=pl.DeviceIdType.MESH)

    def tick(t, carry):
        par, step = decode(t)
        is_fwd = (step >= 0) & (step < chunks)
        is_bwd = (step >= chunks) & (step < 2 * chunks)

        @pl.when(is_fwd)
        def _():
            forward(t, par, step)

        @pl.when(is_bwd)
        def _():
            backward(t, par, step)

        @pl.when(jnp.logical_not(is_fwd | is_bwd))
        def _():
            prefetch_slope(t + 1)

        return carry

    lax.fori_loop(0, tick_count, tick, 0)

    for par in range(2):
        has_out = (me < last) if par == 0 else (me > 0)

        @pl.when(has_out)
        def _():
            drain(obuf.at[par], osem.at[par])

    @pl.when(me == 0)
    def _():
        for hop in range(1, stages):
            drain(sse, lsend.at[hop - 1])
        loss[...] = sse[...]

    @pl.when(me > 0)
    def _():
        drain(sse_in, lsem)
        loss[...] = sse_in[...]


def run_pipeline(stages, seed_scale, tokens, targets, w_in, w_out, gains):
    chunks, rows, d_model = tokens.shape
    d_ff = w_in.shape[2]
    hbm = pl.BlockSpec(memory_space=pl.ANY)
    vmem = pl.BlockSpec(memory_space=pltpu.VMEM)
    out_shape = (
        jax.ShapeDtypeStruct((2, chunks, rows, d_ff), BF16),
        jax.ShapeDtypeStruct((2, chunks, rows, d_ff), BF16),
        jax.ShapeDtypeStruct((2, chunks, rows, d_model), BF16),
        jax.ShapeDtypeStruct((2, chunks, rows, d_model), BF16),
        jax.ShapeDtypeStruct((2, chunks, rows, d_ff), F32),
        jax.ShapeDtypeStruct((2, 8, d_model), F32),
        jax.ShapeDtypeStruct((8, d_model), F32),
    )
    dma = pltpu.SemaphoreType.DMA
    scratch = [
        pltpu.VMEM((2, d_model, d_ff), BF16),
        pltpu.VMEM((2, d_ff, d_model), BF16),
        pltpu.VMEM((2, chunks, rows, d_model), BF16),
        pltpu.VMEM((2, GRAD_SLOTS, rows, d_model), BF16),
        pltpu.VMEM((rows, d_ff), F32),
        pltpu.VMEM((rows, d_ff), BF16),
        pltpu.VMEM((rows, d_model), BF16),
        pltpu.VMEM((2, rows, d_model), BF16),
        pltpu.VMEM((rows, d_model), F32),
        pltpu.VMEM((rows, d_model), BF16),
        pltpu.VMEM((8, d_model), F32),
        pltpu.VMEM((8, d_model), F32),
        dma((2, chunks)), dma((2, chunks)), dma((2,)), pltpu.SemaphoreType.REGULAR((2,)), dma((2, 2)),
        dma, dma, dma, dma, dma, dma, dma((stages - 1,)),
    ]
    flops = 2 * chunks * 8 * rows * d_model * d_ff
    return pl.pallas_call(
        functools.partial(pipeline_kernel, stages, seed_scale),
        out_shape=out_shape,
        in_specs=[hbm, hbm, hbm, hbm, vmem],
        out_specs=(hbm, hbm, hbm, hbm, hbm, vmem, vmem),
        scratch_shapes=scratch,
        compiler_params=pltpu.CompilerParams(
            collective_id=0, has_side_effects=True, vmem_limit_bytes=67043328),
        cost_estimate=pl.CostEstimate(flops=flops, bytes_accessed=16 * chunks * rows * d_ff, transcendentals=0),
        name='pipeline',
    )(tokens, targets, w_in, w_out, gains)


def solution(mesh):
    stages = mesh.shape['stage']

    def device_step(tokens, targets, w_in, w_out, norm_gains):
        micro_count, tokens_mb, d_model = tokens.shape
        d_ff = w_in.shape[2]
        total = micro_count * tokens_mb
        rows = tokens_mb // 2
        chunked = (total // rows, rows, d_model)
        u_st, da_st, n_st, dh_st, _, dgain, sse = run_pipeline(
            stages, 2.0 / total, tokens.reshape(chunked), targets.reshape(chunked),
            w_in, w_out, norm_gains.reshape(2, 1, d_model))
        u_all = u_st.reshape(2, total, d_ff)
        da_all = da_st.reshape(2, total, d_ff)
        n_all = n_st.reshape(2, total, d_model)
        dh_all = dh_st.reshape(2, total, d_model)
        grad_w_in = jnp.einsum('ltd,ltf->ldf', n_all, da_all, preferred_element_type=F32)
        grad_w_out = jnp.einsum('ltf,ltd->lfd', u_all, dh_all, preferred_element_type=F32)
        grad_gains = jnp.sum(dgain, axis=1)
        loss_value = jnp.sum(sse) / (total * d_model)
        return grad_w_in, grad_w_out, grad_gains, loss_value.reshape(1)

    block_spec = P(('dp', 'stage'))
    return jax.shard_map(device_step, mesh=mesh,
                         in_specs=(P('dp'), P('dp'), P('stage'), P('stage'), P('stage')),
                         out_specs=(block_spec, block_spec, block_spec, P('dp')),
                         check_vma=False)
```

time: 3330 us -> 860 us (0.26)
  starting transfers between devices: 1390 us -> 0 us
  matrix products: 1090 us -> 159 us
  Pallas kernels: 0 us -> 694 us
  other arithmetic: 360 us -> 2 us
  local copies, waits for them, and re-layouts: 352 us -> 1.31 us
  loops' own time: 90.2 us -> 0 us
    ppermute x92 -> x0, starting transfers between devices: 1390 us -> none  [the longest x23 1020 us: backward_tick(): recv_up = lax.ppermute(grad_up_out, 'stage', down_perm)]
    dot_general x96 -> x2, matrix products: 1090 us -> 159 us  [the longest x1 79.4 us: device_step(): jnp.einsum('ltd,ltf->ldf', n_all, da_all, preferred_element_type=F32)]
    pallas_call x0 -> x1, Pallas kernels: none -> 694 us  [run_pipeline(): pl.pallas_call(functools.partial(pipeline_kernel, stages, seed_scale), ou...]
    dynamic_slice x115 -> x0, local copies, waits for them, and re-layouts: 165 us -> none  [the longest x46 106 us: store_inputs(): old_rows = lax.dynamic_index_in_dim(buffer_all, mb_index, 1, keepdims=False)]
    dynamic_update_slice x46 -> x0, other arithmetic: 129 us -> none  [the longest x23 87.8 us: store_inputs(): lax.dynamic_update_index_in_dim(buffer_all, jnp.where(is_valid, kept_inpu...]
    select_n x77 -> x0, other arithmetic: 103 us -> none  [the longest x23 31 us: forward_tick(): jnp.where(is_first, lax.dynamic_index_in_dim(tokens, idx_down, 0, keepdim...]
    another operation x94 -> x0, loops' own time: 90.2 us -> none  [the longest x1 55.8 us: device_step(): back_state, _ = lax.scan(backward_tick, back_init, jnp.arange(tick_count))]
    convert_element_type x16 -> x0, other arithmetic: 46.3 us -> none  [layer_backward(): grad_x = (grad_h.astype(jnp.float32) + grad_x_norm).astype(jnp.bfloat16)]
  transfers between devices with their start and end apart: 92 -> 0, of which waited for: 2 -> 0; matrix products, arithmetic and copies ran while one was open for 29% -> 0% of each run, Pallas kernels for 0% -> 0%
where the time goes in v1:
time: 860 us; the launch traced here: 859 us
  Pallas kernels  694 us (81%)
  matrix products  159 us (18%)
    pallas_call x1, Pallas kernels, run_pipeline(): pl.pallas_call(functools.partial(pipeline_kernel, stages, seed_scale), ou...  694 us
    dot_general x1, matrix products, device_step(): jnp.einsum('ltd,ltf->ldf', n_all, da_all, preferred_element_type=F32)  79.4 us
    dot_general x1, matrix products, device_step(): jnp.einsum('ltf,ltd->lfd', u_all, dh_all, preferred_element_type=F32)  79.3 us

profile of v1, /device:TPU:112, one launch (start us, length us, event | category | flops | bytes accessed | tf_op | source)
XLA Modules:
  0.0 858.8 jit_solution(5929039351717634079)
XLA Ops:
  0.6 1.3 reshape.34.gains
  1.9 694.3 %pipeline.1 = (bf16[2,16,256,4096]{3,2,1,0:T(8,128)(2,1)}, bf16[2,16,256,4096]{3,2,1,0:T(8,128)(2,1)}, bf16[2,16,256,1024]{3,2,1,0:T(8,128)(2,1)}, bf16[2,16,256...) custom-call(bf16[16,256,1024]{2,1,0:T(8,128)(2,1)} %bitcast.11, ...), custom_call_target="tpu_custom_call" | custom-call | flops 274877906944 | bytes 268435456 | tf_op jit(solution)/shard_map/pipeline/pallas_call | solution.py:294
  696.3 1.4 reduce_sum.19
  698.3 0.0 copy-start
  698.3 79.4 %fusion = f32[2,1024,4096]{2,1,0:T(8,128)} fusion(bf16[2,4096,1024]{2,1,0:T(8,128)(2,1)} %bitcast.14, bf16[2,4096,4096]{2,1,0:T(8,128)(2,1)} %bitcast.3), kind=kOutput, calls=%fused_computation | convolution fusion | flops 68719476736 | bytes 117440512 | tf_op jit(solution)/shard_map/ltd,ltf->ldf/dot_general | solution.py:323
  777.7 0.0 copy-done
  777.7 0.6 reduce_sum.18
  778.3 79.3 %fusion.1 = f32[2,4096,1024]{2,1,0:T(8,128)} fusion(bf16[2,4096,4096]{2,1,0:T(8,128)(2,1)} %bitcast.4, bf16[2,4096,1024]{2,1,0:T(8,128)(2,1)} %bitcast.13), kind=kOutput, calls=%fused_computation.1 | convolution fusion | flops 68719476736 | bytes 117440512 | tf_op jit(solution)/shard_map/ltf,ltd->lfd/dot_general | solution.py:324
Async XLA Ops:
  698.3 79.4 %copy-start = (f32[2,8,1024]{2,1,0:T(8,128)S(1)}, f32[2,8,1024]{2,1,0:T(8,128)}, u32[]{:S(2)}) copy-start(f32[2,8,1024]{2,1,0:T(8,128)} %get-tuple-element.14) | copy-start | bytes 196612

commit v2 on v1

v2 whole, which is shorter than its diff:
```python
import functools

import jax
import jax.numpy as jnp
from jax import lax
from jax.experimental import pallas as pl
from jax.experimental.pallas import tpu as pltpu
from jax.sharding import PartitionSpec as P

EPSILON = 1e-6
GRAD_SLOTS = 4
HOP_TICKS = 2
TURN_TICKS = 2
GAP = 1
BLOCK = 256
SLAB = 32
KEPT_SLOPE = 4
GELU_C = 0.7978845608028654
GELU_A = 0.044715
F32 = jnp.float32
BF16 = jnp.bfloat16
NT = (((1,), (1,)), ((), ()))


def slope_of(pre):
    sq = pre * pre
    cdf = 0.5 + 0.5 * jnp.tanh(pre * (GELU_C + (GELU_C * GELU_A) * sq))
    hidden = pre * cdf
    return hidden, cdf + (hidden * (1.0 - cdf)) * (2.0 * GELU_C + (6.0 * GELU_C * GELU_A) * sq)


def pipeline_kernel(stages, seed_scale, tokens, targets, w_in, w_out, gains,
                    u_st, da_st, n_st, dh_st, g_st, dgain, loss,
                    wi, wo, xf, bf, gbuf, ubuf, nbuf, obuf, dnbuf, tbuf, sse, sse_in,
                    fsem, bsem, osem, csem, wsem, gsem, usem, nsem, hsem, tsem, lsem, lsend):
    chunks, rows, d_model = tokens.shape
    d_ff = ubuf.shape[1]
    block = min(BLOCK, d_ff // 2)
    blocks = d_ff // block
    slab = min(SLAB, rows // 2)
    wide = d_ff // 2
    half = d_model // 2
    me = lax.axis_index('stage')
    last = stages - 1
    alpha = HOP_TICKS * me
    up_base = 2 * HOP_TICKS * last + TURN_TICKS + 1
    tick_count = up_base + 2 * (2 * chunks - 1 + GAP) + 1
    bwd_from = chunks + GAP

    def drain(ref, sem):
        pltpu.make_async_copy(ref, ref, sem).wait()

    barrier = pltpu.get_barrier_semaphore()
    for hop in range(1, stages):
        pl.semaphore_signal(barrier, inc=1, device_id={'stage': lax.rem(me + hop, stages)},
                            device_id_type=pl.DeviceIdType.MESH)
    pl.semaphore_wait(barrier, stages - 1)

    def load_weights(row):
        pltpu.make_async_copy(w_in.at[row], wi.at[row], wsem.at[0, row]).start()
        pltpu.make_async_copy(w_out.at[row], wo.at[row], wsem.at[1, row]).start()

    def load_tokens(k, carry):
        pltpu.make_async_copy(tokens.at[k], xf.at[0, k], fsem.at[0, k]).start()
        return carry

    @pl.when(me == 0)
    def _():
        load_tokens(0, 0)

    load_weights(0)

    dgain[...] = jnp.zeros(dgain.shape, F32)
    sse[...] = jnp.zeros(sse.shape, F32)

    def decode(t):
        par = lax.rem(t + alpha, 2)
        base = alpha + par * (up_base - 2 * alpha)
        step = lax.div(t - base + 8 * stages, 2) - 4 * stages
        return par, step

    def prefetch_slope(t, h):
        par, step = decode(t)
        cols = slice(h * wide, (h + 1) * wide)

        @pl.when((step >= bwd_from) & (step < bwd_from + chunks))
        def _():
            pltpu.make_async_copy(g_st.at[1 - par, step - bwd_from, :, cols], gbuf.at[:, cols], gsem.at[h]).start()

    def slope_ready(h):
        cols = slice(h * wide, (h + 1) * wide)
        drain(gbuf.at[:, cols], gsem.at[h])

    def forward(t, par, k):
        x_ref = xf.at[par, k]
        sink = (par == 1) & (me == 0)
        turn = (par == 0) & (me == last)
        @pl.when((k > 0) & (((par == 0) & (me < last)) | ((par == 1) & (me > 0))))
        def _():
            drain(obuf.at[par], osem.at[par])

        @pl.when((par == 0) | (me < last))
        def _():
            drain(x_ref, fsem.at[par, k])

        @pl.when(sink)
        def _():
            pltpu.make_async_copy(targets.at[k], tbuf, tsem).start()

        for at in range(0, rows, slab):
            span = slice(at, at + slab)
            x_f32 = x_ref[span, :].astype(F32)
            inv_rms = lax.rsqrt(jnp.mean(x_f32 * x_f32, axis=-1, keepdims=True) + EPSILON)
            nbuf[span, :] = (x_f32 * inv_rms * gains[par]).astype(BF16)
        keep_n = pltpu.make_async_copy(nbuf, n_st.at[par, k], nsem)
        keep_n.start()

        @pl.when(k == 0)
        def _():
            drain(wi.at[par], wsem.at[0, par])
            drain(wo.at[par], wsem.at[1, par])

        @pl.when((k == 0) & (par == 0))
        def _():
            load_weights(1)

            @pl.when(me == 0)
            def _():
                lax.fori_loop(1, chunks, load_tokens, 0)

        def first_dot(j):
            return jnp.dot(nbuf[...], wi[par, :, j * block:(j + 1) * block], preferred_element_type=F32)

        def activate(j, pre):
            cols = slice(j * block, (j + 1) * block)
            if j * 8 < KEPT_SLOPE * blocks:
                hidden, kept = slope_of(pre)
            else:
                sq = pre * pre
                hidden = pre * (0.5 + 0.5 * jnp.tanh(pre * (GELU_C + (GELU_C * GELU_A) * sq)))
                kept = pre
            ubuf[:, cols] = hidden.astype(BF16)
            gbuf[:, cols] = kept

        def second_dot(j):
            cols = slice(j * block, (j + 1) * block)
            part = jnp.dot(ubuf[:, cols], wo[par, cols, :half], preferred_element_type=F32)
            base = x_ref[:, :half].astype(F32) if j == 0 else dnbuf[:, :half]
            total = base + part
            if j == blocks - 1:
                obuf[par, :, :half] = total.astype(BF16)
            else:
                dnbuf[:, :half] = total

        def send_half(cols):
            @pl.when(turn)
            def _():
                xf[1, k, :, cols] = obuf[0, :, cols]

            @pl.when(jnp.logical_not(turn | sink))
            def _():
                pltpu.make_async_remote_copy(
                    src_ref=obuf.at[par, :, cols], dst_ref=xf.at[par, k, :, cols],
                    send_sem=osem.at[par], recv_sem=fsem.at[par, k],
                    device_id={'stage': me + 1 - 2 * par}, device_id_type=pl.DeviceIdType.MESH).start()

        def keep_slope(h):
            cols = slice(h * wide, (h + 1) * wide)
            pltpu.make_async_copy(gbuf.at[:, cols], g_st.at[par, k, :, cols], gsem.at[h]).start()
            pltpu.make_async_copy(ubuf.at[:, cols], u_st.at[par, k, :, cols], usem).start()

        pre = first_dot(0)
        for j in range(blocks):
            activate(j, pre)
            if j + 1 < blocks:
                pre = first_dot(j + 1)
            second_dot(j)
            if j == blocks // 2 - 1:
                keep_slope(0)
        send_half(slice(0, half))
        keep_slope(1)
        slope_ready(0)
        prefetch_slope(t + 1, 0)
        out = x_ref[:, half:].astype(F32) + jnp.dot(ubuf[...], wo[par, :, half:], preferred_element_type=F32)
        obuf[par, :, half:] = out.astype(BF16)
        send_half(slice(half, d_model))
        slope_ready(1)
        prefetch_slope(t + 1, 1)

        @pl.when(sink)
        def _():
            drain(tbuf, tsem)
            error = obuf[1].astype(F32) - tbuf[...].astype(F32)
            sse[...] += jnp.sum((error * error).reshape(rows // 8, 8, d_model), axis=0)
            bf[0, lax.rem(k, GRAD_SLOTS)] = (error * seed_scale).astype(BF16)

            @pl.when(k == chunks - 1)
            def _():
                for hop in range(1, stages):
                    pltpu.make_async_remote_copy(
                        src_ref=sse, dst_ref=sse_in, send_sem=lsend.at[hop - 1], recv_sem=lsem,
                        device_id={'stage': hop}, device_id_type=pl.DeviceIdType.MESH).start()

        keep_n.wait()
        drain(ubuf, usem)

    def backward(t, par, step):
        k = step - bwd_from
        row = 1 - par
        slot = lax.rem(k, GRAD_SLOTS)
        from_peer = ((par == 0) & (me > 0)) | ((par == 1) & (me < last))
        sink = (par == 1) & (me == 0)
        turn = (par == 0) & (me == last)
        remote = jnp.logical_not(sink | turn)
        @pl.when(((par == 0) & (me < last)) | ((par == 1) & (me > 0)))
        def _():
            drain(obuf.at[par], osem.at[par])

        dh_ref = bf.at[par, slot]

        @pl.when(from_peer)
        def _():
            drain(dh_ref, bsem.at[par, k])

        keep_dh = pltpu.make_async_copy(dh_ref, dh_st.at[row, k], hsem)
        keep_dh.start()
        for j in range(blocks):
            if j == 0:
                slope_ready(0)
            if j == blocks // 2:
                slope_ready(1)
            cols = slice(j * block, (j + 1) * block)
            d_hidden = lax.dot_general(dh_ref[...], wo[row, cols, :], NT, preferred_element_type=F32)
            kept = gbuf[:, cols]
            slope = kept if j * 8 < KEPT_SLOPE * blocks else slope_of(kept)[1]
            ubuf[:, cols] = (d_hidden * slope).astype(BF16)
        prefetch_slope(t + 1, 0)
        prefetch_slope(t + 1, 1)
        keep_da = pltpu.make_async_copy(ubuf, da_st.at[row, k], usem)
        keep_da.start()
        for h in range(2):
            cols = slice(h * half, (h + 1) * half)
            dnbuf[:, cols] = lax.dot_general(ubuf[...], wi[row, cols, :], NT, preferred_element_type=F32)

        @pl.when(remote & (k >= GRAD_SLOTS))
        def _():
            pl.semaphore_wait(csem.at[par], 1)

        gain_sum = dgain[row]
        for at in range(0, rows, slab):
            span = slice(at, at + slab)
            x_f32 = xf[row, k, span, :].astype(F32)
            d_normed = dnbuf[span, :]
            inv_rms = lax.rsqrt(jnp.mean(x_f32 * x_f32, axis=-1, keepdims=True) + EPSILON)
            x_hat = x_f32 * inv_rms
            gain_sum = gain_sum + jnp.sum((d_normed * x_hat).reshape(slab // 8, 8, d_model), axis=0)
            scaled = d_normed * gains[row]
            proj = jnp.mean(scaled * x_hat, axis=-1, keepdims=True)
            grad_x = dh_ref[span, :].astype(F32) + inv_rms * (scaled - x_hat * proj)
            obuf[par, span, :] = grad_x.astype(BF16)
            if (at + slab) % (rows // 2) == 0:
                part = slice(at + slab - rows // 2, at + slab)

                @pl.when(remote)
                def _():
                    pltpu.make_async_remote_copy(
                        src_ref=obuf.at[par, part, :], dst_ref=bf.at[par, slot, part, :],
                        send_sem=osem.at[par], recv_sem=bsem.at[par, k],
                        device_id={'stage': me + 1 - 2 * par}, device_id_type=pl.DeviceIdType.MESH).start()
        dgain[row] = gain_sum

        @pl.when(turn)
        def _():
            bf[1, slot] = obuf[0]

        keep_dh.wait()
        keep_da.wait()
        @pl.when(from_peer & (k < chunks - GRAD_SLOTS))
        def _():
            pl.semaphore_signal(csem.at[par], inc=1, device_id={'stage': me - 1 + 2 * par},
                                device_id_type=pl.DeviceIdType.MESH)

    def tick(t, carry):
        par, step = decode(t)
        is_fwd = (step >= 0) & (step < chunks)
        is_bwd = (step >= bwd_from) & (step < bwd_from + chunks)

        @pl.when(is_fwd)
        def _():
            forward(t, par, step)

        @pl.when(is_bwd)
        def _():
            backward(t, par, step)

        @pl.when(jnp.logical_not(is_fwd | is_bwd))
        def _():
            prefetch_slope(t + 1, 0)
            prefetch_slope(t + 1, 1)

        return carry

    lax.fori_loop(0, tick_count, tick, 0)

    for par in range(2):
        has_out = (me < last) if par == 0 else (me > 0)

        @pl.when(has_out)
        def _():
            drain(obuf.at[par], osem.at[par])

    @pl.when(me == 0)
    def _():
        for hop in range(1, stages):
            drain(sse, lsend.at[hop - 1])
        loss[...] = sse[...]

    @pl.when(me > 0)
    def _():
        drain(sse_in, lsem)
        loss[...] = sse_in[...]


def run_pipeline(stages, seed_scale, tokens, targets, w_in, w_out, gains):
    chunks, rows, d_model = tokens.shape
    d_ff = w_in.shape[2]
    hbm = pl.BlockSpec(memory_space=pl.ANY)
    vmem = pl.BlockSpec(memory_space=pltpu.VMEM)
    out_shape = (
        jax.ShapeDtypeStruct((2, chunks, rows, d_ff), BF16),
        jax.ShapeDtypeStruct((2, chunks, rows, d_ff), BF16),
        jax.ShapeDtypeStruct((2, chunks, rows, d_model), BF16),
        jax.ShapeDtypeStruct((2, chunks, rows, d_model), BF16),
        jax.ShapeDtypeStruct((2, chunks, rows, d_ff), F32),
        jax.ShapeDtypeStruct((2, 8, d_model), F32),
        jax.ShapeDtypeStruct((8, d_model), F32),
    )
    dma = pltpu.SemaphoreType.DMA
    scratch = [
        pltpu.VMEM((2, d_model, d_ff), BF16),
        pltpu.VMEM((2, d_ff, d_model), BF16),
        pltpu.VMEM((2, chunks, rows, d_model), BF16),
        pltpu.VMEM((2, GRAD_SLOTS, rows, d_model), BF16),
        pltpu.VMEM((rows, d_ff), F32),
        pltpu.VMEM((rows, d_ff), BF16),
        pltpu.VMEM((rows, d_model), BF16),
        pltpu.VMEM((2, rows, d_model), BF16),
        pltpu.VMEM((rows, d_model), F32),
        pltpu.VMEM((rows, d_model), BF16),
        pltpu.VMEM((8, d_model), F32),
        pltpu.VMEM((8, d_model), F32),
        dma((2, chunks)), dma((2, chunks)), dma((2,)), pltpu.SemaphoreType.REGULAR((2,)), dma((2, 2)),
        dma((2,)), dma, dma, dma, dma, dma, dma((stages - 1,)),
    ]
    flops = 2 * chunks * 8 * rows * d_model * d_ff
    return pl.pallas_call(
        functools.partial(pipeline_kernel, stages, seed_scale),
        out_shape=out_shape,
        in_specs=[hbm, hbm, hbm, hbm, vmem],
        out_specs=(hbm, hbm, hbm, hbm, hbm, vmem, vmem),
        scratch_shapes=scratch,
        compiler_params=pltpu.CompilerParams(
            collective_id=0, has_side_effects=True, vmem_limit_bytes=67043328),
        cost_estimate=pl.CostEstimate(flops=flops, bytes_accessed=16 * chunks * rows * d_ff, transcendentals=0),
        name='pipeline',
    )(tokens, targets, w_in, w_out, gains)


def solution(mesh):
    stages = mesh.shape['stage']

    def device_step(tokens, targets, w_in, w_out, norm_gains):
        micro_count, tokens_mb, d_model = tokens.shape
        d_ff = w_in.shape[2]
        total = micro_count * tokens_mb
        rows = tokens_mb // 2
        chunked = (total // rows, rows, d_model)
        u_st, da_st, n_st, dh_st, _, dgain, sse = run_pipeline(
            stages, 2.0 / total, tokens.reshape(chunked), targets.reshape(chunked),
            w_in, w_out, norm_gains.reshape(2, 1, d_model))
        u_all = u_st.reshape(2, total, d_ff)
        da_all = da_st.reshape(2, total, d_ff)
        n_all = n_st.reshape(2, total, d_model)
        dh_all = dh_st.reshape(2, total, d_model)
        grad_w_in = jnp.einsum('ltd,ltf->ldf', n_all, da_all, preferred_element_type=F32)
        grad_w_out = jnp.einsum('ltf,ltd->lfd', u_all, dh_all, preferred_element_type=F32)
        grad_gains = jnp.sum(dgain, axis=1)
        loss_value = jnp.sum(sse) / (total * d_model)
        return grad_w_in, grad_w_out, grad_gains, loss_value.reshape(1)

    block_spec = P(('dp', 'stage'))
    return jax.shard_map(device_step, mesh=mesh,
                         in_specs=(P('dp'), P('dp'), P('stage'), P('stage'), P('stage')),
                         out_specs=(block_spec, block_spec, block_spec, P('dp')),
                         check_vma=False)
```

time: 860 us -> 767 us (0.89)
  Pallas kernels: 694 us -> 602 us
    pallas_call x1, Pallas kernels: 694 us -> 602 us  [run_pipeline(): pl.pallas_call(functools.partial(pipeline_kernel, stages, seed_scale), ou...]
where the time goes in v2:
time: 767 us
  Pallas kernels  602 us (78%)
  matrix products  159 us (21%)
    pallas_call x1, Pallas kernels, run_pipeline(): pl.pallas_call(functools.partial(pipeline_kernel, stages, seed_scale), ou...  602 us
    dot_general x1, matrix products, device_step(): jnp.einsum('ltd,ltf->ldf', n_all, da_all, preferred_element_type=F32)  79.4 us
    dot_general x1, matrix products, device_step(): jnp.einsum('ltf,ltd->lfd', u_all, dh_all, preferred_element_type=F32)  79.3 us

profile of v2, /device:TPU:112, one launch (start us, length us, event | category | flops | bytes accessed | tf_op | source)
XLA Modules:
  0.0 766.8 jit_solution(14008020626684338046)
XLA Ops:
  0.6 1.3 reshape.34.gains
  1.9 602.4 %pipeline.1 = (bf16[2,16,256,4096]{3,2,1,0:T(8,128)(2,1)}, bf16[2,16,256,4096]{3,2,1,0:T(8,128)(2,1)}, bf16[2,16,256,1024]{3,2,1,0:T(8,128)(2,1)}, bf16[2,16,256...) custom-call(bf16[16,256,1024]{2,1,0:T(8,128)(2,1)} %bitcast.11, ...), custom_call_target="tpu_custom_call" | custom-call | flops 274877906944 | bytes 268435456 | tf_op jit(solution)/shard_map/pipeline/pallas_call | solution.py:356
  604.3 1.4 reduce_sum.19
  606.4 0.0 copy-start
  606.4 79.4 %fusion = f32[2,1024,4096]{2,1,0:T(8,128)} fusion(bf16[2,4096,1024]{2,1,0:T(8,128)(2,1)} %bitcast.14, bf16[2,4096,4096]{2,1,0:T(8,128)(2,1)} %bitcast.3), kind=kOutput, calls=%fused_computation | convolution fusion | flops 68719476736 | bytes 117440512 | tf_op jit(solution)/shard_map/ltd,ltf->ldf/dot_general | solution.py:385
  685.8 0.0 copy-done
  685.8 0.6 reduce_sum.18
  686.4 79.3 %fusion.1 = f32[2,4096,1024]{2,1,0:T(8,128)} fusion(bf16[2,4096,4096]{2,1,0:T(8,128)(2,1)} %bitcast.4, bf16[2,4096,1024]{2,1,0:T(8,128)(2,1)} %bitcast.13), kind=kOutput, calls=%fused_computation.1 | convolution fusion | flops 68719476736 | bytes 117440512 | tf_op jit(solution)/shard_map/ltf,ltd->lfd/dot_general | solution.py:386
Async XLA Ops:
  606.4 79.4 %copy-start = (f32[2,8,1024]{2,1,0:T(8,128)S(1)}, f32[2,8,1024]{2,1,0:T(8,128)}, u32[]{:S(2)}) copy-start(f32[2,8,1024]{2,1,0:T(8,128)} %get-tuple-element.14) | copy-start | bytes 196612
